TPU v7x, 32 devices: a whole 2x2x4 slice. The times are simulated.
32 devices in a mesh: section: 4 (over x, core), tensor: 4 (over z), dp: 2 (over y).
Axes of the slice: x: 2, y: 2, z: 4, core: 2. Of those that a mesh axis runs over, the one named last changes fastest.
Arguments:
- layer_in: bfloat16 [2, 2, 4, 2, 128, 2560], P(None, None, 'section', 'dp', 'tensor'), may hold values from -6 to 6
- carry_in: bfloat16 [2, 4, 2, 128, 2560], P(None, 'section', 'dp', 'tensor'), may hold values from -6 to 6
- top_grad: bfloat16 [1, 2, 128, 2560], P(None, 'dp', 'tensor'), may hold values from -6 to 6
- w_qkv: bfloat16 [2, 4, 2560, 2560], P(None, 'section', None, 'tensor'), may hold values from -1 to 1
- w_out: bfloat16 [2, 4, 2048, 2560], P(None, 'section', 'tensor'), may hold values from -0.125 to 0.125
- gain: float32 [2, 4, 2560], P(None, 'section'), may hold values from 0.5 to 1.5
Outputs:
- unit_grads: bfloat16 [2, 2, 4, 2, 128, 2560], P(None, None, 'section', 'dp', 'tensor')
- grad_qkv: bfloat16 [2, 4, 2560, 2560], P(None, 'section', 'dp', 'tensor')
- grad_out: bfloat16 [2, 4, 2048, 2560], P(None, 'section', ('tensor', 'dp'))
- grad_gain: float32 [2, 4, 2560], P(None, 'section')
All inputs are finite; a program needn't handle non-finite values.
Results may differ from a plain program's by a relative error of at most 0.022.
The roundings to bfloat16 on the way count: a program that leaves them out, or rounds other values in their place, can miss the bound.
Values may be sent and summed in bfloat16 or wider, within the bound.
A program may use at most 128 MiB of HBM per device.

v0:
```python
import math
import jax
import jax.numpy as jnp
from jax import lax
from jax.sharding import PartitionSpec as P

KV = 4
HD = 64
GROUP = 8
epsilon = 1e-06
rope_base = 1000000.0


def from_behind(value, axis, steps):
    count = lax.axis_size(axis)
    first, last = (max(0, -steps), min(count, count - steps))
    return lax.ppermute(value, axis, [(source, source + steps) for source in range(first, last)])


def rope_tables(length, head_width):
    half_width = head_width // 2
    exponent = jnp.arange(half_width, dtype=jnp.float32) * (2.0 / head_width)
    frequency = rope_base ** (-exponent)
    angle = jnp.arange(length, dtype=jnp.float32)[:, None] * frequency[None, :]
    return (jnp.cos(angle), jnp.sin(angle))


def rotate(values, cosine_table, sine_table, direction):
    half_width = values.shape[-1] // 2
    table_shape = (values.shape[0],) + (1,) * (values.ndim - 2) + (half_width,)
    cosine = cosine_table.reshape(table_shape)
    sine_part = direction * sine_table.reshape(table_shape)
    lower_half = values[..., :half_width]
    upper_half = values[..., half_width:]
    return jnp.concatenate(
        [
            lower_half * cosine - upper_half * sine_part,
            upper_half * cosine + lower_half * sine_part,
        ],
        axis=-1,
    )


def local(layer_in, carry_in, top_grad, w_qkv, w_out, gain):
    ticks = layer_in.shape[0]
    own_rows = layer_in.shape[4]
    length = own_rows * lax.axis_size("tensor")
    kv_local = KV // lax.axis_size("tensor")
    section_index = lax.axis_index("section")
    at_first = section_index == 0
    at_last = section_index == lax.axis_size("section") - 1
    cosine_table, sine_table = rope_tables(length, HD)
    score_scale = 1.0 / math.sqrt(HD)
    causal_mask = jnp.arange(length)[:, None] >= jnp.arange(length)[None, :]
    layer_rows = layer_in[:, :, 0, 0]
    carried = carry_in[:, 0, 0]
    fresh_grads = top_grad[:, 0]
    weight_qkv = w_qkv[:, 0]
    weight_out = w_out[:, 0]
    gain_rows = gain[:, 0]
    contract_rows = (((0,), (0,)), ((), ()))
    contract_cols = (((1,), (1,)), ((), ()))
    qkv_sums = [
        jnp.zeros(weight_qkv.shape[1:], jnp.float32),
        jnp.zeros(weight_qkv.shape[1:], jnp.float32),
    ]
    out_sums = [
        jnp.zeros(weight_out.shape[1:], jnp.float32),
        jnp.zeros(weight_out.shape[1:], jnp.float32),
    ]
    gain_totals = [
        jnp.zeros(gain_rows.shape[1:], jnp.float32),
        jnp.zeros(gain_rows.shape[1:], jnp.float32),
    ]

    def apply_weights(member, stored):
        normed, grad_full, attended, grad_projected = stored
        qkv_sums[member] = qkv_sums[member] + lax.dot_general(
            normed, grad_projected, contract_rows, preferred_element_type=jnp.float32
        )
        out_sums[member] = out_sums[member] + lax.dot_general(
            attended, grad_full, contract_rows, preferred_element_type=jnp.float32
        )

    inputs = [carried[0], carried[1]]
    per_tick = []
    for position in range(ticks):
        outcome = [None, None]
        pending_members = []
        pending_saved = []
        for member in (1, 0):
            layer_part = layer_rows[position, member]
            grad_output = inputs[member]
            inputs_float = layer_part.astype(jnp.float32)
            inverse = lax.rsqrt(
                jnp.mean(inputs_float * inputs_float, axis=-1, keepdims=True) + epsilon
            )
            unit_rows = inputs_float * inverse
            normed_own = (unit_rows * gain_rows[member]).astype(jnp.bfloat16)
            input_normed = lax.all_gather(normed_own, "tensor", axis=0, tiled=True)
            input_grad_full = lax.all_gather(grad_output, "tensor", axis=0, tiled=True)
            projected = jnp.dot(
                input_normed, weight_qkv[member], preferred_element_type=jnp.float32
            )
            projected = projected.reshape(length, kv_local, GROUP + 2, HD)
            query_rot = rotate(projected[:, :, :GROUP], cosine_table, sine_table, 1.0).astype(
                jnp.bfloat16
            )
            key_rot = rotate(projected[:, :, GROUP], cosine_table, sine_table, 1.0).astype(
                jnp.bfloat16
            )
            value_rows = projected[:, :, GROUP + 1].astype(jnp.bfloat16)
            scores = (
                jnp.einsum("tkgd,ukd->kgtu", query_rot, key_rot, preferred_element_type=jnp.float32)
                * score_scale
            )
            scores = jnp.where(causal_mask, scores, -1e30)
            exponentials = jnp.exp(scores - jnp.max(scores, axis=-1, keepdims=True))
            softmax_rows = exponentials / jnp.sum(exponentials, axis=-1, keepdims=True)
            softmax_low = softmax_rows.astype(jnp.bfloat16)
            input_attended = jnp.einsum(
                "kgtu,ukd->tkgd", softmax_low, value_rows, preferred_element_type=jnp.float32
            )
            input_attended = input_attended.astype(jnp.bfloat16).reshape(
                length, kv_local * GROUP * HD
            )
            grad_attended = lax.dot_general(
                input_grad_full,
                weight_out[member],
                contract_cols,
                preferred_element_type=jnp.float32,
            ).astype(jnp.bfloat16)
            grad_heads = grad_attended.reshape(length, kv_local, GROUP, HD)
            grad_softmax = jnp.einsum(
                "tkgd,ukd->kgtu", grad_heads, value_rows, preferred_element_type=jnp.float32
            )
            row_total = jnp.sum(softmax_rows * grad_softmax, axis=-1, keepdims=True)
            grad_scores = (softmax_rows * (grad_softmax - row_total) * score_scale).astype(
                jnp.bfloat16
            )
            grad_value = jnp.einsum(
                "kgtu,tkgd->ukd", softmax_low, grad_heads, preferred_element_type=jnp.float32
            )
            grad_query = rotate(
                jnp.einsum(
                    "kgtu,ukd->tkgd", grad_scores, key_rot, preferred_element_type=jnp.float32
                ),
                cosine_table,
                sine_table,
                -1.0,
            )
            grad_key = rotate(
                jnp.einsum(
                    "kgtu,tkgd->ukd", grad_scores, query_rot, preferred_element_type=jnp.float32
                ),
                cosine_table,
                sine_table,
                -1.0,
            )
            input_grad_projected = jnp.concatenate(
                [grad_query, grad_key[:, :, None], grad_value[:, :, None]], axis=2
            )
            input_grad_projected = input_grad_projected.reshape(
                length, kv_local * (GROUP + 2) * HD
            ).astype(jnp.bfloat16)
            grad_normed = lax.psum_scatter(
                lax.dot_general(
                    input_grad_projected,
                    weight_qkv[member],
                    contract_cols,
                    preferred_element_type=jnp.float32,
                ).astype(jnp.bfloat16),
                "tensor",
                scatter_dimension=0,
                tiled=True,
            ).astype(jnp.float32)
            grad_unit = grad_normed * gain_rows[member]
            grad_rows = inverse * (
                grad_unit - unit_rows * jnp.mean(grad_unit * unit_rows, axis=-1, keepdims=True)
            )
            grad_input = (grad_output.astype(jnp.float32) + grad_rows).astype(jnp.bfloat16)
            grad_scale = jnp.sum(grad_normed * unit_rows, axis=0)
            grad_input, stored, grad_scale = (
                grad_input,
                (input_normed, input_grad_full, input_attended, input_grad_projected),
                grad_scale,
            )
            outcome[member] = grad_input
            gain_totals[member] = gain_totals[member] + grad_scale
            pending_members.append(member)
            pending_saved.append(stored)
        if position + 1 < ticks:
            upward = from_behind(outcome[1], "section", 1)
            downward = from_behind(outcome[0], "section", -1)
            pending_saved, upward, downward = lax.optimization_barrier(
                (pending_saved, upward, downward)
            )
            inputs = [
                jnp.where(at_last, outcome[1], downward),
                jnp.where(at_first, fresh_grads[position], upward),
            ]
        for member, stored in zip(pending_members, pending_saved):
            apply_weights(member, stored)
        per_tick.append(jnp.stack(outcome))
    grad_qkv_all, grad_out_all = (
        lax.psum_scatter(
            jnp.stack(qkv_sums).astype(jnp.bfloat16), "dp", scatter_dimension=1, tiled=True
        ).astype(jnp.float32),
        lax.psum_scatter(
            jnp.stack(out_sums).astype(jnp.bfloat16), "dp", scatter_dimension=1, tiled=True
        ).astype(jnp.float32),
    )
    gain_total = lax.psum(jnp.stack(gain_totals), ("tensor", "dp"))
    unit_grads = jnp.stack(per_tick)[:, :, None, None]
    return (
        unit_grads,
        grad_qkv_all.astype(jnp.bfloat16)[:, None],
        grad_out_all.astype(jnp.bfloat16)[:, None],
        gain_total[:, None],
    )


def solution(mesh):
    in_specs = (
        P(None, None, "section", "dp", "tensor", None),
        P(None, "section", "dp", "tensor", None),
        P(None, "dp", "tensor", None),
        P(None, "section", None, "tensor"),
        P(None, "section", "tensor", None),
        P(None, "section", None),
    )
    out_specs = (
        P(None, None, "section", "dp", "tensor", None),
        P(None, "section", "dp", "tensor"),
        P(None, "section", ("tensor", "dp"), None),
        P(None, "section", None),
    )
    return jax.shard_map(local, mesh=mesh, in_specs=in_specs, out_specs=out_specs, check_vma=False)
```

profile of v0, /device:TPU:0, one launch (start us, length us, event | category | flops | bytes accessed | tf_op | source)
XLA Modules:
  0.0 479.4 jit_solution(15156333436391977317)
XLA Ops:
  11.8 19.7 %all-gather = bf16[1,1,1,128,2560]{4,3,2,1,0:T(8,128)(2,1)S(1)} all-gather(bf16[1,1,1,32,2560]{4,3,2,1,0:T(8,128)(2,1)S(1)} %get-tuple-element.68), channel_id=2, replica_groups=mesh['section'=4,'tensor'=4,'dp'=2] {'tensor'}, dimensions={3}, use_global_device_ids=true | all-gather | bytes 819200 | tf_op jit(solution)/shard_map/all_gather | solution.py:101
  32.3 2.7 fusion.32
  35.4 17.5 %all_gather.24 = bf16[128,2560]{1,0:T(8,128)(2,1)} all-gather(bf16[32,2560]{1,0:T(8,128)(2,1)S(1)} %get-tuple-element.58), channel_id=1, replica_groups=mesh['section'=4,'tensor'=4,'dp'=2] {'tensor'}, dimensions={0}, use_global_device_ids=true | all-gather | bytes 819200 | tf_op jit(solution)/shard_map/all_gather | solution.py:100
  52.9 16.7 %all_gather.26 = bf16[128,2560]{1,0:T(8,128)(2,1)} all-gather(bf16[32,2560]{1,0:T(8,128)(2,1)S(1)} %get-tuple-element.59), channel_id=1, replica_groups=mesh['section'=4,'tensor'=4,'dp'=2] {'tensor'}, dimensions={0}, use_global_device_ids=true | all-gather | bytes 819200 | tf_op jit(solution)/shard_map/all_gather | solution.py:100
  69.6 6.2 %slice_bitcast_fusion.1 = (bf16[640,2560]{0,1:T(8,128)(2,1)}, bf16[640,2560]{0,1:T(8,128)(2,1)}) fusion(bf16[2,1,2560,640]{3,2,1,0:T(8,128)(2,1)} %param.9), kind=kLoop, calls=%fused_computation.30 | loop fusion | bytes 13107200 | tf_op jit(solution)/shard_map/dot_general | solution.py:102
  75.9 4.0 copy.39
  79.9 2.1 convolution_bitcast_fusion.7
  82.7 5.7 %copy.44 = bf16[640,2560]{1,0:T(8,128)(2,1)} copy(bf16[640,2560]{0,1:T(8,128)(2,1)} %get-tuple-element.51) | data formatting | bytes 6553600 | tf_op jit(solution)/shard_map/dot_general | solution.py:102
  88.4 3.2 convolution_bitcast_fusion.6
  95.4 15.2 %all-gather.1 = bf16[1,1,1,128,2560]{4,3,2,1,0:T(8,128)(2,1)S(1)} all-gather(bf16[1,1,1,32,2560]{4,3,2,1,0:T(8,128)(2,1)S(1)} %copy-done.33), channel_id=3, replica_groups=mesh['section'=4,'tensor'=4,'dp'=2] {'tensor'}, dimensions={3}, use_global_device_ids=true | all-gather | bytes 819200 | tf_op jit(solution)/shard_map/all_gather | solution.py:101
  111.5 3.4 fusion.38
  123.0 4.0 convolution_convert_fusion.2
  129.2 4.0 convolution_convert_fusion.3
  137.2 13.4 %reduce-scatter.9.cloned.1.call-done = bf16[32,2560]{1,0:T(8,128)(2,1)} async-done(((bf16[128,2560]{1,0:T(8,128)(2,1)}), bf16[32,2560]{1,0:T(8,128)(2,1)}) %reduce-scatter.9.cloned.1.call-update) | async-done | bytes 163856 | tf_op jit(solution)/shard_map/reduce_scatter | solution.py:166
  150.5 24.1 %reduce-scatter.7.cloned.1.call-done = bf16[32,2560]{1,0:T(8,128)(2,1)} async-done(((bf16[128,2560]{1,0:T(8,128)(2,1)}), bf16[32,2560]{1,0:T(8,128)(2,1)}) %reduce-scatter.7.cloned.1.call-update) | async-done | bytes 163856 | tf_op jit(solution)/shard_map/reduce_scatter | solution.py:166
  174.7 2.3 fusion.90
  178.8 16.5 %all_gather.30 = bf16[128,2560]{1,0:T(8,128)(2,1)S(1)} all-gather(bf16[32,2560]{1,0:T(8,128)(2,1)S(1)} %get-tuple-element.54), channel_id=1, replica_groups=mesh['section'=4,'tensor'=4,'dp'=2] {'tensor'}, dimensions={0}, use_global_device_ids=true | all-gather | bytes 819200 | tf_op jit(solution)/shard_map/all_gather | solution.py:100
  196.4 15.8 %all_gather.28 = bf16[128,2560]{1,0:T(8,128)(2,1)S(1)} all-gather(bf16[32,2560]{1,0:T(8,128)(2,1)S(1)} %get-tuple-element.55), channel_id=1, replica_groups=mesh['section'=4,'tensor'=4,'dp'=2] {'tensor'}, dimensions={0}, use_global_device_ids=true | all-gather | bytes 819200 | tf_op jit(solution)/shard_map/all_gather | solution.py:100
  214.8 3.0 collective-permute-start
  221.0 17.3 %all_gather.29 = bf16[128,2560]{1,0:T(8,128)(2,1)S(1)} all-gather(bf16[32,2560]{1,0:T(8,128)(2,1)S(1)} %broadcast_select_fusion), channel_id=1, replica_groups=mesh['section'=4,'tensor'=4,'dp'=2] {'tensor'}, dimensions={0}, use_global_device_ids=true | all-gather | bytes 819200 | tf_op jit(solution)/shard_map/all_gather | solution.py:101
  244.0 16.7 %all_gather.31 = bf16[128,2560]{1,0:T(8,128)(2,1)S(1)} all-gather(bf16[32,2560]{1,0:T(8,128)(2,1)S(1)} %bitcast_select_fusion), channel_id=1, replica_groups=mesh['section'=4,'tensor'=4,'dp'=2] {'tensor'}, dimensions={0}, use_global_device_ids=true | all-gather | bytes 819200 | tf_op jit(solution)/shard_map/all_gather | solution.py:101
  261.5 3.5 fusion.41
  272.2 2.0 convolution_convert_fusion
  277.3 4.0 convolution_convert_fusion.1
  281.2 3.2 fusion.189
  284.5 3.4 fusion.3
  289.9 2.7 pad_maximum_fusion.1
  298.0 3.4 pad_maximum_fusion
  302.5 19.2 %reduce-scatter.11.cloned.1.call-done = bf16[32,2560]{1,0:T(8,128)(2,1)} async-done(((bf16[128,2560]{1,0:T(8,128)(2,1)}), bf16[32,2560]{1,0:T(8,128)(2,1)}) %reduce-scatter.11.cloned.1.call-update) | async-done | bytes 163856 | tf_op jit(solution)/shard_map/reduce_scatter | solution.py:166
  323.2 36.0 %psum.7 = f32[2,1,2560]{2,1,0:T(1,128)} all-reduce(f32[2,1,2560]{2,1,0:T(1,128)S(1)} %broadcast_in_dim.33), channel_id=1, replica_groups=mesh['section'=4,'tensor'=4,'dp'=2] {'tensor','dp'}, use_global_device_ids=true, to_apply=%region_30.31 | all-reduce | flops 5120 | bytes 40960 | tf_op jit(solution)/shard_map/psum | solution.py:213
  361.4 28.5 %reduce-scatter.17.cloned.1.call-done = bf16[2,256,2560]{2,1,0:T(8,128)(2,1)} async-done(((bf16[2,512,2560]{2,1,0:T(8,128)(2,1)}), bf16[2,256,2560]{2,1,0:T(8,128)(2,1)}) %reduce-scatter.17.cloned.1.call-update) | async-done | bytes 2621456 | tf_op jit(solution)/shard_map/reduce_scatter | solution.py:209
  389.9 82.6 %reduce-scatter.15.cloned.1.call-done = bf16[2,1280,640]{2,1,0:T(8,128)(2,1)} async-done(((bf16[2,2560,640]{2,1,0:T(8,128)(2,1)}), bf16[2,1280,640]{2,1,0:T(8,128)(2,1)}) %reduce-scatter.15.cloned.1.call-update) | async-done | bytes 3276816 | tf_op jit(solution)/shard_map/reduce_scatter | solution.py:206
  (319 shorter events, 61.7 us)
Async XLA Ops:
  7.2 28.0 %copy-start.1 = (bf16[2,2,1,1,32,2560]{5,4,3,2,1,0:T(8,128)(2,1)S(1)}, bf16[2,2,1,1,32,2560]{5,4,3,2,1,0:T(8,128)(2,1)}, u32[]{:S(2)}) copy-start(bf16[2,2,1,1,32,2560]{5,4,3,2,1,0:T(8,128)(2,1)} %param.6) | copy-start | bytes 1966084
  7.2 143.4 %reduce-scatter.9.cloned.1.call-start = ((), (), s32[]{:S(2)}) async-start(), calls=%async_computation.7 | async-start | bytes 819200 | tf_op jit(solution)/shard_map/reduce_scatter | solution.py:166
  7.2 84.4 %copy-start.88 = (f32[32]{0:T(128)}, f32[32]{0:T(128)S(1)}, u32[]{:S(2)}) copy-start(f32[32]{0:T(128)S(1)} %negate_power_fusion) | copy-start | bytes 388
  7.3 85.9 %copy-start.49 = (pred[128,128]{0,1:T(8,128)(4,1)}, pred[128,128]{0,1:T(8,128)(4,1)S(1)}, u32[]{:S(2)}) copy-start(pred[128,128]{0,1:T(8,128)(4,1)S(1)} %iota_compare_fusion) | copy-start | bytes 49156
  9.3 26.1 %copy-start.42 = (f32[2560]{0:T(1024)}, f32[2560]{0:T(1024)S(1)}, u32[]{:S(2)}) copy-start(f32[2560]{0:T(1024)S(1)} %get-tuple-element.49) | copy-start | bytes 30724
  10.1 82.3 %copy-start.45 = (f32[128,32]{0,1:T(8,128)}, f32[128,32]{0,1:T(8,128)S(1)}, u32[]{:S(2)}) copy-start(f32[128,32]{0,1:T(8,128)S(1)} %get-tuple-element.112) | copy-start | bytes 49156
  10.1 82.3 %copy-start.59 = (f32[128,32]{0,1:T(8,128)}, f32[128,32]{0,1:T(8,128)S(1)}, u32[]{:S(2)}) copy-start(f32[128,32]{0,1:T(8,128)S(1)} %get-tuple-element.111) | copy-start | bytes 49156
  35.1 58.4 %copy-start.63 = (bf16[128,512]{0,1:T(8,128)(2,1)}, bf16[128,512]{0,1:T(8,128)(2,1)S(1)}, u32[]{:S(2)}) copy-start(bf16[128,512]{0,1:T(8,128)(2,1)S(1)} %copy.40) | copy-start | bytes 393220
  35.2 40.7 %copy-start.92 = (f32[32]{0:T(128)}, f32[32]{0:T(128)S(1)}, u32[]{:S(2)}) copy-start(f32[32]{0:T(128)S(1)} %get-tuple-element.129) | copy-start | bytes 388
  35.2 40.7 %copy-start.94 = (f32[32]{0:T(128)}, f32[32]{0:T(128)S(1)}, u32[]{:S(2)}) copy-start(f32[32]{0:T(128)S(1)} %get-tuple-element.130) | copy-start | bytes 388
  127.0 47.6 %reduce-scatter.7.cloned.1.call-start = ((), (), s32[]{:S(2)}) async-start(), calls=%async_computation.6 | async-start | bytes 819200 | tf_op jit(solution)/shard_map/reduce_scatter | solution.py:166
  133.1 41.5 %copy-start.43 = (f32[2560]{0:T(1024)S(1)}, f32[2560]{0:T(1024)}, u32[]{:S(2)}) copy-start(f32[2560]{0:T(1024)} %copy-done.42) | copy-start | bytes 30724
  133.2 41.5 %copy-start.93 = (f32[32]{0:T(128)S(1)}, f32[32]{0:T(128)}, u32[]{:S(2)}) copy-start(f32[32]{0:T(128)} %copy-done.92) | copy-start | bytes 388
  133.2 41.5 %copy-start.95 = (f32[32]{0:T(128)S(1)}, f32[32]{0:T(128)}, u32[]{:S(2)}) copy-start(f32[32]{0:T(128)} %copy-done.94) | copy-start | bytes 388
  133.2 169.3 %reduce-scatter.13.cloned.1.call-start = ((), (), s32[]{:S(2)}) async-start(), calls=%async_computation.9 | async-start | bytes 819200 | tf_op jit(solution)/shard_map/reduce_scatter | solution.py:166
  174.7 20.7 %copy-start = (bf16[640,2560]{1,0:T(8,128)(2,1)S(1)}, bf16[640,2560]{1,0:T(8,128)(2,1)}, u32[]{:S(2)}) copy-start(bf16[640,2560]{1,0:T(8,128)(2,1)} %copy.44) | copy-start | bytes 9830404
  178.8 34.6 %copy-start.31 = (bf16[32,2560]{1,0:T(8,128)(2,1)}, bf16[32,2560]{1,0:T(8,128)(2,1)S(1)}, u32[]{:S(2)}) copy-start(bf16[32,2560]{1,0:T(8,128)(2,1)S(1)} %get-tuple-element.52) | copy-start | bytes 491524
  178.8 41.5 %copy-start.19 = (bf16[32,2560]{1,0:T(8,128)(2,1)}, bf16[32,2560]{1,0:T(8,128)(2,1)S(1)}, u32[]{:S(2)}) copy-start(bf16[32,2560]{1,0:T(8,128)(2,1)S(1)} %get-tuple-element.53) | copy-start | bytes 491524
  195.3 43.9 %slice-start.2 = ((s8[5242880]{0:T(1024)(128)(4,1)}), s8[1048576]{0:T(1024)(128)(4,1)S(1)}, s32[]{:S(2)}) async-start(s8[5242880]{0:T(1024)(128)(4,1)} %bitcast.493), calls=%async_computation.14 | async-start | bytes 2097152
  196.4 21.4 %copy-start.90 = (f32[32]{0:T(128)S(1)}, f32[32]{0:T(128)}, u32[]{:S(2)}) copy-start(f32[32]{0:T(128)} %copy-done.88) | copy-start | bytes 388
  196.4 21.6 %copy-start.50 = (pred[128,128]{0,1:T(8,128)(4,1)S(1)}, pred[128,128]{0,1:T(8,128)(4,1)}, u32[]{:S(2)}) copy-start(pred[128,128]{0,1:T(8,128)(4,1)} %copy-done.49) | copy-start | bytes 49156
  212.2 27.1 %slice-start.3 = ((s8[5242880]{0:T(1024)(128)(4,1)}), s8[4194304]{0:T(1024)(128)(4,1)S(1)}, s32[]{:S(2)}) async-start(s8[5242880]{0:T(1024)(128)(4,1)} %bitcast.493), calls=%async_computation.15 | async-start | bytes 8388608
  213.4 6.9 %collective-permute-start.1 = (bf16[32,2560]{1,0:T(8,128)(2,1)S(1)}, bf16[32,2560]{1,0:T(8,128)(2,1)S(1)}, u32[]{:S(2)}, u32[]{:S(2)}) collective-permute-start(bf16[32,2560]{1,0:T(8,128)(2,1)S(1)} %get-tuple-element.52), channel_id=1, source_target_pairs={{8,0},{16,8},{24,16},{9,1},{17,9},{25,17},{10,2},{18,10},{26,18},{... | collective-permute-start | bytes 491528 | tf_op jit(solution)/shard_map/ppermute | solution.py:17
  214.8 5.5 %collective-permute-start = (bf16[32,2560]{1,0:T(8,128)(2,1)S(1)}, bf16[32,2560]{1,0:T(8,128)(2,1)S(1)}, u32[]{:S(2)}, u32[]{:S(2)}) collective-permute-start(bf16[32,2560]{1,0:T(8,128)(2,1)S(1)} %get-tuple-element.53), channel_id=1, source_target_pairs={{0,8},{8,16},{16,24},{1,9},{9,17},{17,25},{2,10},{10,18},{18,26},{... | collective-permute-start | bytes 491528 | tf_op jit(solution)/shard_map/ppermute | solution.py:17
  218.4 23.0 %copy-start.84 = (f32[8,128]{1,0:T(8,128)}, f32[8,128]{1,0:T(8,128)S(1)}, u32[]{:S(2)}) copy-start(f32[8,128]{1,0:T(8,128)S(1)} %fusion.53) | copy-start | bytes 12292
  274.2 47.5 %reduce-scatter.11.cloned.1.call-start = ((), (), s32[]{:S(2)}) async-start(), calls=%async_computation.8 | async-start | bytes 819200 | tf_op jit(solution)/shard_map/reduce_scatter | solution.py:166
  284.4 105.5 %reduce-scatter.17.cloned.1.call-start = ((), (), s32[]{:S(2)}) async-start(), calls=%async_computation.11 | async-start | bytes 7864320 | tf_op jit(solution)/shard_map/reduce_scatter | solution.py:209
  292.6 179.9 %reduce-scatter.15.cloned.1.call-start = ((), (), s32[]{:S(2)}) async-start(), calls=%async_computation.10 | async-start | bytes 9830400 | tf_op jit(solution)/shard_map/reduce_scatter | solution.py:206
  301.4 21.6 %copy-start.75 = (f32[2560]{0:T(1024)S(1)}, f32[2560]{0:T(1024)}, u32[]{:S(2)}) copy-start(f32[2560]{0:T(1024)} %get-tuple-element.43) | copy-start | bytes 30724
  301.4 21.7 %copy-start.74 = (f32[2560]{0:T(1024)S(1)}, f32[2560]{0:T(1024)}, u32[]{:S(2)}) copy-start(f32[2560]{0:T(1024)} %get-tuple-element.34) | copy-start | bytes 30724
  301.5 57.7 %copy-start.22 = (bf16[32,2560]{1,0:T(8,128)(2,1)S(1)}, bf16[32,2560]{1,0:T(8,128)(2,1)}, u32[]{:S(2)}) copy-start(bf16[32,2560]{1,0:T(8,128)(2,1)} %copy-done.21) | copy-start | bytes 491524
  301.5 57.7 %copy-start.24 = (bf16[32,2560]{1,0:T(8,128)(2,1)S(1)}, bf16[32,2560]{1,0:T(8,128)(2,1)}, u32[]{:S(2)}) copy-start(bf16[32,2560]{1,0:T(8,128)(2,1)} %copy-done.23) | copy-start | bytes 491524
  (80 other events, 446.7 us)
Sparse Core Ops, SparseCore 0:
  127.1 23.3 reduce-scatter.8
  153.4 21.2 reduce-scatter.6
  274.4 23.2 reduce-scatter.12
  300.4 21.2 reduce-scatter.10
  324.4 65.4 reduce-scatter.16
  392.6 79.8 reduce-scatter.14
where the time goes:
time: 481 us; the launch traced here: 479 us
  blocking collectives  171 us (36%)
  waiting for transfers between devices  168 us (35%)
  matrix products  64 us (13%)
  local copies, waits for them, and re-layouts  32.3 us (7%)
  other arithmetic  23 us (5%)
  between operations  15.6 us (3%)
  starting transfers between devices  4.93 us (1%)
    reduce_scatter x1, waiting for transfers between devices, local(): lax.psum_scatter(jnp.stack(qkv_sums).astype(jnp.bfloat16), 'dp', scatter_...  82.6 us
    all_gather x4, blocking collectives, local(): input_grad_full = lax.all_gather(grad_output, 'tensor', axis=0, tiled=True)  68.9 us
    all_gather x4, blocking collectives, local(): input_normed = lax.all_gather(normed_own, 'tensor', axis=0, tiled=True)  66.6 us
    reduce_scatter x4, waiting for transfers between devices, local(): lax.psum_scatter(lax.dot_general(input_grad_projected, weight_qkv[member]...  56.8 us
    psum x1, blocking collectives, local(): gain_total = lax.psum(jnp.stack(gain_totals), ('tensor', 'dp'))  36 us
    reduce_scatter x1, waiting for transfers between devices, local(): lax.psum_scatter(jnp.stack(out_sums).astype(jnp.bfloat16), 'dp', scatter_...  28.5 us
    dot_general x3, local copies, waits for them, and re-layouts, local(): jnp.dot(input_normed, weight_qkv[member], preferred_element_type=jnp.floa...  15.9 us
    dot_general x4, matrix products, local(): lax.dot_general(input_grad_projected, weight_qkv[member], contract_cols,...  14 us
  transfers between devices with their start and end apart: 8, of which 5 were waited for; matrix products, arithmetic and copies ran while one was open for 8% of the time, Pallas kernels for 0%

commit v1 on v0

--- a/solution.py
+++ b/solution.py
@@ -9,6 +9,22 @@
 GROUP = 8
 epsilon = 1e-06
 rope_base = 1000000.0
+
+
+def _pack_racks(q_in, peer_axis, dim_k=0):
+    p_count = lax.psum(1, peer_axis)
+    by_place = list(map(lambda idx: (idx, (idx + 1) % p_count), range(p_count)))
+
+    def tokens_save(current_block):
+        if len(current_block) == p_count:
+            return current_block
+        return tokens_save([lax.ppermute(current_block[0], peer_axis, by_place), *current_block])
+
+    return jnp.roll(
+        jnp.concatenate(tokens_save([q_in]), axis=dim_k),
+        shift=(lax.axis_index(peer_axis) + 1) * q_in.shape[dim_k],
+        axis=dim_k,
+    )
 
 
 def from_behind(value, axis, steps):
@@ -97,7 +113,7 @@
             )
             unit_rows = inputs_float * inverse
             normed_own = (unit_rows * gain_rows[member]).astype(jnp.bfloat16)
-            input_normed = lax.all_gather(normed_own, "tensor", axis=0, tiled=True)
+            input_normed = _pack_racks(normed_own, "tensor")
             input_grad_full = lax.all_gather(grad_output, "tensor", axis=0, tiled=True)
             projected = jnp.dot(
                 input_normed, weight_qkv[member], preferred_element_type=jnp.float32

time: 481 us -> 437 us (0.909)
  blocking collectives: 171 us -> 117 us
  matrix products: 64 us -> 50.9 us
  waiting for transfers between devices: 168 us -> 179 us
  starting transfers between devices: 4.93 us -> 14.8 us
  other arithmetic: 23 us -> 28.7 us
    all_gather x4 -> x0, blocking collectives: 66.6 us -> none  [local(): input_normed = lax.all_gather(normed_own, 'tensor', axis=0, tiled=True)]
    all_gather x4, blocking collectives: 68.9 us -> 80.7 us  [local(): input_grad_full = lax.all_gather(grad_output, 'tensor', axis=0, tiled=True)]
    ppermute x0 -> x12, waiting for transfers between devices: none -> 10.8 us  [tokens_save(): lax.ppermute(current_block[0], peer_axis, by_place)]
    ppermute x0 -> x12, starting transfers between devices: none -> 9.65 us  [tokens_save(): lax.ppermute(current_block[0], peer_axis, by_place)]
    concatenate x0 -> x4, other arithmetic: none -> 9.63 us  [_pack_racks(): jnp.roll(jnp.concatenate(tokens_save([q_in]), axis=dim_k), shift=(lax.axi...]
    unnamed x208 -> x132, local copies, waits for them, and re-layouts: 10.3 us -> 8 us
  transfers between devices with their start and end apart: 8 -> 20, of which waited for: 5 -> 8; matrix products, arithmetic and copies ran while one was open for 8% -> 18% of each run, Pallas kernels for 0% -> 0%
where the time goes in v1:
time: 437 us; the launch traced here: 436 us
  waiting for transfers between devices  179 us (41%)
  blocking collectives  117 us (27%)
  matrix products  50.9 us (12%)
  local copies, waits for them, and re-layouts  30.9 us (7%)
  other arithmetic  28.7 us (7%)
  between operations  15.3 us (4%)
  starting transfers between devices  14.8 us (3%)
    reduce_scatter x1, waiting for transfers between devices, local(): lax.psum_scatter(jnp.stack(qkv_sums).astype(jnp.bfloat16), 'dp', scatter_...  82.6 us
    all_gather x4, blocking collectives, local(): input_grad_full = lax.all_gather(grad_output, 'tensor', axis=0, tiled=True)  80.7 us
    reduce_scatter x4, waiting for transfers between devices, local(): lax.psum_scatter(lax.dot_general(input_grad_projected, weight_qkv[member]...  56.6 us
    psum x1, blocking collectives, local(): gain_total = lax.psum(jnp.stack(gain_totals), ('tensor', 'dp'))  36 us
    reduce_scatter x1, waiting for transfers between devices, local(): lax.psum_scatter(jnp.stack(out_sums).astype(jnp.bfloat16), 'dp', scatter_...  28.5 us
    dot_general x3, local copies, waits for them, and re-layouts, local(): jnp.dot(input_normed, weight_qkv[member], preferred_element_type=jnp.floa...  16.2 us
    dot_general x4, matrix products, local(): lax.dot_general(input_grad_projected, weight_qkv[member], contract_cols,...  12.1 us
    ppermute x12, waiting for transfers between devices, tokens_save(): lax.ppermute(current_block[0], peer_axis, by_place)  10.8 us
  transfers between devices with their start and end apart: 20, of which 8 were waited for; matrix products, arithmetic and copies ran while one was open for 18% of the time, Pallas kernels for 0%

profile of v1, /device:TPU:0, one launch (start us, length us, event | category | flops | bytes accessed | tf_op | source)
XLA Modules:
  0.0 435.9 jit_solution(9172819786857363509)
XLA Ops:
  10.4 3.1 collective-permute-start
  16.1 18.9 %all-gather = bf16[1,1,1,128,2560]{4,3,2,1,0:T(8,128)(2,1)S(1)} all-gather(bf16[1,1,1,32,2560]{4,3,2,1,0:T(8,128)(2,1)S(1)} %get-tuple-element.69), channel_id=2, replica_groups=mesh['section'=4,'tensor'=4,'dp'=2] {'tensor'}, dimensions={3}, use_global_device_ids=true | all-gather | bytes 819200 | tf_op jit(solution)/shard_map/all_gather | solution.py:117
  35.0 6.5 %slice_bitcast_fusion.1 = (bf16[640,2560]{0,1:T(8,128)(2,1)}, bf16[640,2560]{0,1:T(8,128)(2,1)}) fusion(bf16[2,1,2560,640]{3,2,1,0:T(8,128)(2,1)} %param.11), kind=kLoop, calls=%fused_computation.30 | loop fusion | bytes 13107200 | tf_op jit(solution)/shard_map/dot_general | solution.py:118
  42.5 17.1 %all-gather.1 = bf16[1,1,1,128,2560]{4,3,2,1,0:T(8,128)(2,1)S(1)} all-gather(bf16[1,1,1,32,2560]{4,3,2,1,0:T(8,128)(2,1)S(1)} %get-tuple-element.70), channel_id=3, replica_groups=mesh['section'=4,'tensor'=4,'dp'=2] {'tensor'}, dimensions={3}, use_global_device_ids=true | all-gather | bytes 819200 | tf_op jit(solution)/shard_map/all_gather | solution.py:117
  62.3 5.6 %collective-permute-done.1 = bf16[32,2560]{1,0:T(8,128)(2,1)} collective-permute-done((bf16[32,2560]{1,0:T(8,128)(2,1)S(1)}, bf16[32,2560]{1,0:T(8,128)(2,1)}, u32[]{:S(2)}, u32[]{:S(2)}) %collective-permute-start.1) | collective-permute-done | bytes 163872 | tf_op jit(solution)/shard_map/ppermute | solution.py:21
  69.6 4.0 copy.39
  73.6 5.7 %copy.44 = bf16[640,2560]{1,0:T(8,128)(2,1)} copy(bf16[640,2560]{0,1:T(8,128)(2,1)} %get-tuple-element.52) | data formatting | bytes 6553600 | tf_op jit(solution)/shard_map/dot_general | solution.py:118
  79.4 2.4 fusion.68
  82.9 3.8 collective-permute-done.5
  86.7 2.4 fusion.61
  99.0 4.0 convolution_convert_fusion.3
  105.3 15.5 %reduce-scatter.9.cloned.1.call-done = bf16[32,2560]{1,0:T(8,128)(2,1)} async-done(((bf16[128,2560]{1,0:T(8,128)(2,1)}), bf16[32,2560]{1,0:T(8,128)(2,1)}) %reduce-scatter.9.cloned.1.call-update) | async-done | bytes 163856 | tf_op jit(solution)/shard_map/reduce_scatter | solution.py:182
  120.7 24.1 %reduce-scatter.7.cloned.1.call-done = bf16[32,2560]{1,0:T(8,128)(2,1)} async-done(((bf16[128,2560]{1,0:T(8,128)(2,1)}), bf16[32,2560]{1,0:T(8,128)(2,1)}) %reduce-scatter.7.cloned.1.call-update) | async-done | bytes 163856 | tf_op jit(solution)/shard_map/reduce_scatter | solution.py:182
  147.3 2.2 fusion.115
  150.9 3.0 collective-permute-start.6
  157.7 22.4 %all_gather.15 = bf16[128,2560]{1,0:T(8,128)(2,1)S(1)} all-gather(bf16[32,2560]{1,0:T(8,128)(2,1)S(1)} %bitcast_select_fusion), channel_id=1, replica_groups=mesh['section'=4,'tensor'=4,'dp'=2] {'tensor'}, dimensions={0}, use_global_device_ids=true | all-gather | bytes 819200 | tf_op jit(solution)/shard_map/all_gather | solution.py:117
  180.9 3.4 fusion.41
  187.3 22.3 %all_gather.14 = bf16[128,2560]{1,0:T(8,128)(2,1)S(1)} all-gather(bf16[32,2560]{1,0:T(8,128)(2,1)} %broadcast_select_fusion), channel_id=1, replica_groups=mesh['section'=4,'tensor'=4,'dp'=2] {'tensor'}, dimensions={0}, use_global_device_ids=true | all-gather | bytes 819200 | tf_op jit(solution)/shard_map/all_gather | solution.py:117
  210.5 3.4 fusion.35
  217.3 2.4 fusion.47
  219.7 3.2 convolution_bitcast_fusion.4
  223.0 2.4 fusion.54
  230.9 2.0 convolution_convert_fusion
  234.3 4.0 convolution_convert_fusion.1
  238.4 3.2 fusion.216
  241.8 3.6 fusion.2
  248.5 2.8 pad_maximum_fusion.1
  256.8 3.4 pad_maximum_fusion
  261.2 17.0 %reduce-scatter.11.cloned.1.call-done = bf16[32,2560]{1,0:T(8,128)(2,1)} async-done(((bf16[128,2560]{1,0:T(8,128)(2,1)}), bf16[32,2560]{1,0:T(8,128)(2,1)}) %reduce-scatter.11.cloned.1.call-update) | async-done | bytes 163856 | tf_op jit(solution)/shard_map/reduce_scatter | solution.py:182
  279.7 36.0 %psum.7 = f32[2,1,2560]{2,1,0:T(1,128)} all-reduce(f32[2,1,2560]{2,1,0:T(1,128)S(1)} %broadcast_in_dim.33), channel_id=1, replica_groups=mesh['section'=4,'tensor'=4,'dp'=2] {'tensor','dp'}, use_global_device_ids=true, to_apply=%region_30.32 | all-reduce | flops 5120 | bytes 40960 | tf_op jit(solution)/shard_map/psum | solution.py:229
  318.0 28.5 %reduce-scatter.17.cloned.1.call-done = bf16[2,256,2560]{2,1,0:T(8,128)(2,1)} async-done(((bf16[2,512,2560]{2,1,0:T(8,128)(2,1)}), bf16[2,256,2560]{2,1,0:T(8,128)(2,1)}) %reduce-scatter.17.cloned.1.call-update) | async-done | bytes 2621456 | tf_op jit(solution)/shard_map/reduce_scatter | solution.py:225
  346.4 82.6 %reduce-scatter.15.cloned.1.call-done = bf16[2,1280,640]{2,1,0:T(8,128)(2,1)} async-done(((bf16[2,2560,640]{2,1,0:T(8,128)(2,1)}), bf16[2,1280,640]{2,1,0:T(8,128)(2,1)}) %reduce-scatter.15.cloned.1.call-update) | async-done | bytes 3276816 | tf_op jit(solution)/shard_map/reduce_scatter | solution.py:222
  (268 shorter events, 59.6 us)
Async XLA Ops:
  7.2 113.6 %reduce-scatter.9.cloned.1.call-start = ((), (), s32[]{:S(2)}) async-start(), calls=%async_computation.7 | async-start | bytes 819200 | tf_op jit(solution)/shard_map/reduce_scatter | solution.py:182
  10.4 31.2 %copy-start.30 = (bf16[32,2560]{1,0:T(8,128)(2,1)}, bf16[32,2560]{1,0:T(8,128)(2,1)S(1)}, u32[]{:S(2)}) copy-start(bf16[32,2560]{1,0:T(8,128)(2,1)S(1)} %get-tuple-element.59) | copy-start | bytes 491524
  10.4 49.2 %collective-permute-start = (bf16[32,2560]{1,0:T(8,128)(2,1)S(1)}, bf16[32,2560]{1,0:T(8,128)(2,1)S(1)}, u32[]{:S(2)}, u32[]{:S(2)}) collective-permute-start(bf16[32,2560]{1,0:T(8,128)(2,1)S(1)} %get-tuple-element.59), channel_id=1, source_target_pairs={{0,2},{2,4},{4,6},{6,0},{1,3},{3,5},{5,7},{7,1},{8,10},{10,12},{12... | collective-permute-start | bytes 491528 | tf_op jit(solution)/shard_map/ppermute | solution.py:21
  13.5 48.5 %collective-permute-start.3 = (bf16[32,2560]{1,0:T(8,128)(2,1)S(1)}, bf16[32,2560]{1,0:T(8,128)(2,1)}, u32[]{:S(2)}, u32[]{:S(2)}) collective-permute-start(bf16[32,2560]{1,0:T(8,128)(2,1)S(1)} %get-tuple-element.60), channel_id=1, source_target_pairs={{0,2},{2,4},{4,6},{6,0},{1,3},{3,5},{5,7},{7,1},{8,10},{10,12},{12... | collective-permute-start | bytes 491528 | tf_op jit(solution)/shard_map/ppermute | solution.py:21
  16.1 25.4 %slice-start.4 = ((s8[5242880]{0:T(1024)(128)(4,1)}), s8[4194304]{0:T(1024)(128)(4,1)S(1)}, s32[]{:S(2)}) async-start(s8[5242880]{0:T(1024)(128)(4,1)} %bitcast.495), calls=%async_computation.16 | async-start | bytes 8388608
  59.6 8.3 %collective-permute-start.1 = (bf16[32,2560]{1,0:T(8,128)(2,1)S(1)}, bf16[32,2560]{1,0:T(8,128)(2,1)}, u32[]{:S(2)}, u32[]{:S(2)}) collective-permute-start(bf16[32,2560]{1,0:T(8,128)(2,1)S(1)} %collective-permute-done), channel_id=1, source_target_pairs={{0,2},{2,4},{4,6},{6,0},{1,3},{3,5},{5,7},{7,1},{8,10},{10,12},{12... | collective-permute-start | bytes 491528 | tf_op jit(solution)/shard_map/ppermute | solution.py:21
  62.0 32.0 %copy-start.50 = (f32[32]{0:T(128)}, f32[32]{0:T(128)S(1)}, u32[]{:S(2)}) copy-start(f32[32]{0:T(128)S(1)} %negate_power_fusion) | copy-start | bytes 388
  62.0 17.4 %collective-permute-start.4 = (bf16[32,2560]{1,0:T(8,128)(2,1)}, bf16[32,2560]{1,0:T(8,128)(2,1)}, u32[]{:S(2)}, u32[]{:S(2)}) collective-permute-start(bf16[32,2560]{1,0:T(8,128)(2,1)} %collective-permute-done.3), channel_id=1, source_target_pairs={{0,2},{2,4},{4,6},{6,0},{1,3},{3,5},{5,7},{7,1},{8,10},{10,12},{12... | collective-permute-start | bytes 491528 | tf_op jit(solution)/shard_map/ppermute | solution.py:21
  67.9 11.5 %collective-permute-start.2 = (bf16[32,2560]{1,0:T(8,128)(2,1)}, bf16[32,2560]{1,0:T(8,128)(2,1)}, u32[]{:S(2)}, u32[]{:S(2)}) collective-permute-start(bf16[32,2560]{1,0:T(8,128)(2,1)} %collective-permute-done.1), channel_id=1, source_target_pairs={{0,2},{2,4},{4,6},{6,0},{1,3},{3,5},{5,7},{7,1},{8,10},{10,12},{12... | collective-permute-start | bytes 491528 | tf_op jit(solution)/shard_map/ppermute | solution.py:21
  79.4 7.4 %collective-permute-start.5 = (bf16[32,2560]{1,0:T(8,128)(2,1)}, bf16[32,2560]{1,0:T(8,128)(2,1)S(1)}, u32[]{:S(2)}, u32[]{:S(2)}) collective-permute-start(bf16[32,2560]{1,0:T(8,128)(2,1)} %collective-permute-done.4), channel_id=1, source_target_pairs={{0,2},{2,4},{4,6},{6,0},{1,3},{3,5},{5,7},{7,1},{8,10},{10,12},{12... | collective-permute-start | bytes 491528 | tf_op jit(solution)/shard_map/ppermute | solution.py:21
  96.9 47.9 %reduce-scatter.7.cloned.1.call-start = ((), (), s32[]{:S(2)}) async-start(), calls=%async_computation.6 | async-start | bytes 819200 | tf_op jit(solution)/shard_map/reduce_scatter | solution.py:182
  103.0 41.9 %copy-start.53 = (f32[32]{0:T(128)S(1)}, f32[32]{0:T(128)}, u32[]{:S(2)}) copy-start(f32[32]{0:T(128)} %copy-done.52) | copy-start | bytes 388
  103.0 41.9 %copy-start.55 = (f32[32]{0:T(128)S(1)}, f32[32]{0:T(128)}, u32[]{:S(2)}) copy-start(f32[32]{0:T(128)} %copy-done.54) | copy-start | bytes 388
  103.0 158.2 %reduce-scatter.13.cloned.1.call-start = ((), (), s32[]{:S(2)}) async-start(), calls=%async_computation.9 | async-start | bytes 819200 | tf_op jit(solution)/shard_map/reduce_scatter | solution.py:182
  144.9 9.1 %copy-start.12 = (f32[1,8,128,128]{2,3,1,0:T(8,128)S(1)}, f32[1,8,128,128]{2,3,1,0:T(8,128)}, u32[]{:S(2)}) copy-start(f32[1,8,128,128]{2,3,1,0:T(8,128)} %copy-done.11) | copy-start | bytes 1572868
  149.5 30.6 %copy-start.28 = (bf16[32,2560]{1,0:T(8,128)(2,1)}, bf16[32,2560]{1,0:T(8,128)(2,1)S(1)}, u32[]{:S(2)}) copy-start(bf16[32,2560]{1,0:T(8,128)(2,1)S(1)} %get-tuple-element.53) | copy-start | bytes 491524
  149.5 7.5 %collective-permute-start.7 = (bf16[32,2560]{1,0:T(8,128)(2,1)S(1)}, bf16[32,2560]{1,0:T(8,128)(2,1)S(1)}, u32[]{:S(2)}, u32[]{:S(2)}) collective-permute-start(bf16[32,2560]{1,0:T(8,128)(2,1)S(1)} %get-tuple-element.53), channel_id=1, source_target_pairs={{8,0},{16,8},{24,16},{9,1},{17,9},{25,17},{10,2},{18,10},{26,18},{... | collective-permute-start | bytes 491528 | tf_op jit(solution)/shard_map/ppermute | solution.py:33
  150.9 6.1 %collective-permute-start.6 = (bf16[32,2560]{1,0:T(8,128)(2,1)S(1)}, bf16[32,2560]{1,0:T(8,128)(2,1)S(1)}, u32[]{:S(2)}, u32[]{:S(2)}) collective-permute-start(bf16[32,2560]{1,0:T(8,128)(2,1)S(1)} %get-tuple-element.54), channel_id=1, source_target_pairs={{0,8},{8,16},{16,24},{1,9},{9,17},{17,25},{2,10},{10,18},{18,26},{... | collective-permute-start | bytes 491528 | tf_op jit(solution)/shard_map/ppermute | solution.py:33
  155.6 30.3 %collective-permute-start.11 = (bf16[32,2560]{1,0:T(8,128)(2,1)}, bf16[32,2560]{1,0:T(8,128)(2,1)}, u32[]{:S(2)}, u32[]{:S(2)}) collective-permute-start(bf16[32,2560]{1,0:T(8,128)(2,1)} %get-tuple-element.55), channel_id=1, source_target_pairs={{0,2},{2,4},{4,6},{6,0},{1,3},{3,5},{5,7},{7,1},{8,10},{10,12},{12... | collective-permute-start | bytes 491528 | tf_op jit(solution)/shard_map/ppermute | solution.py:21
  155.6 30.4 %collective-permute-start.8 = (bf16[32,2560]{1,0:T(8,128)(2,1)}, bf16[32,2560]{1,0:T(8,128)(2,1)}, u32[]{:S(2)}, u32[]{:S(2)}) collective-permute-start(bf16[32,2560]{1,0:T(8,128)(2,1)} %get-tuple-element.56), channel_id=1, source_target_pairs={{0,2},{2,4},{4,6},{6,0},{1,3},{3,5},{5,7},{7,1},{8,10},{10,12},{12... | collective-permute-start | bytes 491528 | tf_op jit(solution)/shard_map/ppermute | solution.py:21
  186.0 23.7 %collective-permute-start.12 = (bf16[32,2560]{1,0:T(8,128)(2,1)}, bf16[32,2560]{1,0:T(8,128)(2,1)}, u32[]{:S(2)}, u32[]{:S(2)}) collective-permute-start(bf16[32,2560]{1,0:T(8,128)(2,1)} %collective-permute-done.11), channel_id=1, source_target_pairs={{0,2},{2,4},{4,6},{6,0},{1,3},{3,5},{5,7},{7,1},{8,10},{10,12},{12... | collective-permute-start | bytes 491528 | tf_op jit(solution)/shard_map/ppermute | solution.py:21
  186.0 29.5 %collective-permute-start.9 = (bf16[32,2560]{1,0:T(8,128)(2,1)}, bf16[32,2560]{1,0:T(8,128)(2,1)}, u32[]{:S(2)}, u32[]{:S(2)}) collective-permute-start(bf16[32,2560]{1,0:T(8,128)(2,1)} %collective-permute-done.8), channel_id=1, source_target_pairs={{0,2},{2,4},{4,6},{6,0},{1,3},{3,5},{5,7},{7,1},{8,10},{10,12},{12... | collective-permute-start | bytes 491528 | tf_op jit(solution)/shard_map/ppermute | solution.py:21
  209.7 7.7 %collective-permute-start.13 = (bf16[32,2560]{1,0:T(8,128)(2,1)}, bf16[32,2560]{1,0:T(8,128)(2,1)}, u32[]{:S(2)}, u32[]{:S(2)}) collective-permute-start(bf16[32,2560]{1,0:T(8,128)(2,1)} %collective-permute-done.12), channel_id=1, source_target_pairs={{0,2},{2,4},{4,6},{6,0},{1,3},{3,5},{5,7},{7,1},{8,10},{10,12},{12... | collective-permute-start | bytes 491528 | tf_op jit(solution)/shard_map/ppermute | solution.py:21
  215.5 7.4 %collective-permute-start.10 = (bf16[32,2560]{1,0:T(8,128)(2,1)}, bf16[32,2560]{1,0:T(8,128)(2,1)S(1)}, u32[]{:S(2)}, u32[]{:S(2)}) collective-permute-start(bf16[32,2560]{1,0:T(8,128)(2,1)} %collective-permute-done.9), channel_id=1, source_target_pairs={{0,2},{2,4},{4,6},{6,0},{1,3},{3,5},{5,7},{7,1},{8,10},{10,12},{12... | collective-permute-start | bytes 491528 | tf_op jit(solution)/shard_map/ppermute | solution.py:21
  233.0 45.3 %reduce-scatter.11.cloned.1.call-start = ((), (), s32[]{:S(2)}) async-start(), calls=%async_computation.8 | async-start | bytes 819200 | tf_op jit(solution)/shard_map/reduce_scatter | solution.py:182
  241.6 104.9 %reduce-scatter.17.cloned.1.call-start = ((), (), s32[]{:S(2)}) async-start(), calls=%async_computation.11 | async-start | bytes 7864320 | tf_op jit(solution)/shard_map/reduce_scatter | solution.py:225
  251.3 177.8 %reduce-scatter.15.cloned.1.call-start = ((), (), s32[]{:S(2)}) async-start(), calls=%async_computation.10 | async-start | bytes 9830400 | tf_op jit(solution)/shard_map/reduce_scatter | solution.py:222
  260.2 18.0 %copy-start.2 = (bf16[2,2,1,1,32,2560]{5,4,3,2,1,0:T(8,128)(2,1)S(1)}, bf16[2,2,1,1,32,2560]{5,4,3,2,1,0:T(8,128)(2,1)}, u32[]{:S(2)}) copy-start(bf16[2,2,1,1,32,2560]{5,4,3,2,1,0:T(8,128)(2,1)} %param.8) | copy-start | bytes 1966084
  260.2 18.0 %copy-start.57 = (f32[32]{0:T(128)S(1)}, f32[32]{0:T(128)}, u32[]{:S(2)}) copy-start(f32[32]{0:T(128)} %copy-done.56) | copy-start | bytes 388
  260.2 18.0 %copy-start.59 = (f32[32]{0:T(128)S(1)}, f32[32]{0:T(128)}, u32[]{:S(2)}) copy-start(f32[32]{0:T(128)} %copy-done.58) | copy-start | bytes 388
  260.3 55.5 %copy-start.22 = (bf16[32,2560]{1,0:T(8,128)(2,1)S(1)}, bf16[32,2560]{1,0:T(8,128)(2,1)}, u32[]{:S(2)}) copy-start(bf16[32,2560]{1,0:T(8,128)(2,1)} %copy-done.21) | copy-start | bytes 491524
  260.3 55.5 %copy-start.23 = (bf16[32,2560]{1,0:T(8,128)(2,1)S(1)}, bf16[32,2560]{1,0:T(8,128)(2,1)}, u32[]{:S(2)}) copy-start(bf16[32,2560]{1,0:T(8,128)(2,1)} %broadcast_select_fusion) | copy-start | bytes 491524
  (54 other events, 131.8 us)
Sparse Core Ops, SparseCore 0:
  97.1 23.6 reduce-scatter.8
  123.6 21.2 reduce-scatter.6
  233.1 21.1 reduce-scatter.12
  257.0 21.2 reduce-scatter.10
  281.0 65.4 reduce-scatter.16
  349.1 79.8 reduce-scatter.14
